TPU v7x, 256 devices: a whole 4x4x8 slice. The times are simulated.
256 devices in a mesh: gz: 32 (over y, z), gy: 4 (over x), gx: 2 (over core).
Axes of the slice: x: 4, y: 4, z: 8, core: 2. Of those that a mesh axis runs over, the one named last changes fastest.
Arguments:
- right_side: float32 [256, 64, 256], P('gz', 'gy', 'gx'), may hold values from -128 to 128
- diagonal: float32 [256, 64, 256], P('gz', 'gy', 'gx'), may hold values from 0.05 to 1
Outputs:
- solution_field: float32 [256, 64, 256], P('gz', 'gy', 'gx')
- residual: float32 [256, 64, 256], P('gz', 'gy', 'gx')
All inputs are finite; a program needn't handle non-finite values.
Results may differ from a plain program's by a relative error of at most 0.03.
Values sent between devices are 32-bit elements.
A program may use at most 64 MiB of HBM per device.

v0:
```python
import jax
import jax.numpy as jnp
import numpy as np
from jax import lax
from jax.experimental import pallas as pl
from jax.experimental.pallas import tpu as pltpu
from jax.sharding import PartitionSpec as P

S = 6
OUTER = 5
COLS = 2 * S + 1
SHIFT = 19.0
HALF = 19.0
LANES = 128
ROWS = 8
MESH = pl.DeviceIdType.MESH


def basis_change():
    matrix = np.zeros((COLS, COLS), np.float32)
    for offset, length in ((0, S), (S + 1, S - 1)):
        for degree in range(length):
            matrix[offset + degree, offset + degree] = SHIFT
            if degree == 0:
                matrix[offset + 1, offset] = HALF
            else:
                matrix[offset + degree + 1, offset + degree] = 0.5 * HALF
                matrix[offset + degree - 1, offset + degree] = 0.5 * HALF
    return matrix


def table(index, values):
    out = jnp.zeros(index.shape, jnp.float32)
    for position, value in enumerate(values):
        if value:
            out = jnp.where(index == position, jnp.float32(value), out)
    return out


def kernel(nz, ny, nx, rhs_ref, diag_ref, sol_out, res_out,
           fields, p_chain, r_chain, scale2, weight, total, pairs, g_send, g_recv, final,
           z_send, z_recv, y_send, y_recv, g_ssem, g_rsem, swap_send, swap_recv, own_sem):
    bz, by, bx = rhs_ref.shape
    hy = by // 2
    ze, halves, ya = fields.shape[1:4]
    first = (ya - hy) // 2
    low_rows, high_rows = slice(first - ROWS, first), slice(first + hy, first + hy + ROWS)
    iz, iy, ix = lax.axis_index("gz"), lax.axis_index("gy"), lax.axis_index("gx")
    other = 1 - ix
    yy = iy * 2 + ix
    count = nz * ny * nx
    me = (iz * ny + iy) * nx + ix
    has_z = (iz > 0, iz < nz - 1)
    has_y = (yy > 0, yy < 2 * ny - 1)
    z_dev = tuple((iz + s, iy, ix) for s in (-1, 1))
    y_dev = tuple((iz, (yy + s) // 2, other) for s in (-1, 1))
    mid_z, mid_y = slice(S, S + bz), slice(first, first + hy)

    def row_tile(index):
        return pl.ds(pl.multiple_of(index * hy, hy), hy)

    swaps, owns = [], []
    for k, ref in enumerate((rhs_ref, diag_ref)):
        spot = fields.at[1 + k, mid_z, ix, mid_y, :]
        swap = pltpu.make_async_remote_copy(
            src_ref=ref.at[:, row_tile(other), :], dst_ref=spot,
            send_sem=swap_send.at[k], recv_sem=swap_recv.at[k],
            device_id=(iz, iy, other), device_id_type=MESH)
        swap.start()
        own = pltpu.make_async_copy(ref.at[:, row_tile(ix), :], spot, own_sem.at[k])
        own.start()
        swaps.append(swap)
        owns.append(own)

    for side in range(2):
        planes = slice(0, S) if side == 0 else slice(S + bz, ze)
        rows = (low_rows, high_rows)[side]

        @pl.when(jnp.logical_not(has_z[side]))
        def _():
            for k in (0, 1, 2):
                fields[k, planes] = jnp.zeros((S, halves, ya, bx), jnp.float32)

        @pl.when(jnp.logical_not(has_y[side]))
        def _():
            for k in (0, 1, 2):
                fields[k, :, :, rows, :] = jnp.zeros((ze, halves, ROWS, bx), jnp.float32)

    w_unit = 2.0 / HALF
    w_low = jnp.where(has_y[0], jnp.float32(w_unit), 0.0)
    w_high = jnp.where(has_y[1], jnp.float32(w_unit), 0.0)
    z_low = jnp.where(has_z[0], jnp.float32(1.0), 0.0)
    z_high = jnp.where(has_z[1], jnp.float32(1.0), 0.0)
    for plane in range(ze):
        factor = z_low if plane < S else (z_high if plane >= S + bz else jnp.float32(1.0))
        for tile, w in enumerate((w_low, jnp.float32(w_unit), w_high)):
            weight[plane, tile] = jnp.broadcast_to(w * factor, (ROWS, bx))
    total[...] = jnp.zeros(total.shape, jnp.float32)
    pairs[...] = jnp.zeros(pairs.shape, jnp.float32)

    for copy in owns + swaps:
        copy.wait()

    def z_copy(item, side):
        field, depth, k = item
        low_src, high_src = slice(S, S + depth), slice(S + bz - depth, S + bz)
        low_dst, high_dst = slice(S - depth, S), slice(S + bz, S + bz + depth)
        src, dst = ((low_src, high_dst), (high_src, low_dst))[side]
        return pltpu.make_async_remote_copy(
            src_ref=fields.at[field, src, :, mid_y, :], dst_ref=fields.at[field, dst, :, mid_y, :],
            send_sem=z_send.at[k, side], recv_sem=z_recv.at[k, 1 - side],
            device_id=z_dev[side], device_id_type=MESH)

    def y_copy(item, side, part):
        field, depth, k = item
        planes = (mid_z, slice(S - depth, S), slice(S + bz, S + bz + depth))[part]
        low_src, high_src = slice(first, first + depth), slice(first + hy - depth, first + hy)
        low_dst, high_dst = slice(first - depth, first), slice(first + hy, first + hy + depth)
        src, dst = ((low_src, high_dst), (high_src, low_dst))[side]
        return pltpu.make_async_remote_copy(
            src_ref=fields.at[field, planes, :, src, :], dst_ref=fields.at[field, planes, :, dst, :],
            send_sem=y_send.at[k, side, part], recv_sem=y_recv.at[k, 1 - side, part],
            device_id=y_dev[side], device_id_type=MESH)

    def exchange(shallow):
        items = ((1, S, 0), (shallow, S - 1, 1))
        for item in items:
            for side in range(2):
                @pl.when(has_z[side])
                def _():
                    z_copy(item, side).start()
        for item in items:
            for side in range(2):
                @pl.when(has_y[side])
                def _():
                    y_copy(item, side, 0).start()
        for item in items:
            for z_side in range(2):
                @pl.when(has_z[z_side])
                def _():
                    z_copy(item, 1 - z_side).wait_recv()
                    for side in range(2):
                        @pl.when(has_y[side])
                        def _():
                            y_copy(item, side, 1 + z_side).start()
        for item in items:
            for side in range(2):
                @pl.when(has_z[side])
                def _():
                    z_copy(item, side).wait_send()

                @pl.when(has_y[side])
                def _():
                    y_copy(item, side, 0).wait_send()
                    y_copy(item, 1 - side, 0).wait_recv()
                    for z_side in range(2):
                        @pl.when(has_z[z_side])
                        def _():
                            y_copy(item, side, 1 + z_side).wait_send()
                            y_copy(item, 1 - side, 1 + z_side).wait_recv()

    exchange(2)
    all_rows = slice(first - ROWS, first + hy + ROWS)

    def prepare(plane, c):
        fields[0, plane] = fields[1, plane]
        scale2[plane] = (fields[2, plane, :, all_rows, :] + (27.0 - SHIFT)) * (2.0 / HALF)
        return c
    lax.fori_loop(0, ze, prepare, 0)

    tiles = (hy + 2 * ROWS) // ROWS
    lane_id = lax.broadcasted_iota(jnp.int32, (ROWS, bx), 1)
    first_lane, last_lane = lane_id == 0, lane_id == bx - 1

    def row_sums(ref, z, tile):
        at = first - ROWS + tile * ROWS
        return [ref[z, h, at - 1:at - 1 + ROWS, :] + ref[z, h, at:at + ROWS, :] + ref[z, h, at + 1:at + 1 + ROWS, :]
                for h in range(halves)]

    def lane_sums(parts):
        left = [pltpu.roll(v, 1, 1) for v in parts]
        right = [pltpu.roll(v, bx - 1, 1) for v in parts]
        out = []
        for h in range(halves):
            before = left[h - 1] if h else 0.0
            after = right[h + 1] if h < halves - 1 else 0.0
            out.append(parts[h] + jnp.where(first_lane, before, left[h]) + jnp.where(last_lane, after, right[h]))
        return out

    p_at = [fields.at[1]] + [p_chain.at[k] for k in range(S)]
    r_at = [fields.at[0]] + [r_chain.at[k] for k in range(S - 1)]

    def degree_sweep(chains, degree, start, stop, chosen):
        jobs = [(chain, tile) for chain in chains for tile in chosen]

        def step(z, carry):
            out = []
            for (chain, tile), (before, here) in zip(jobs, carry):
                after = row_sums(chain[degree], z + 1, tile)
                box = lane_sums([a + b + c for a, b, c in zip(before, here, after)])
                at = first - ROWS + tile * ROWS
                for h in range(halves):
                    value = (scale2[z, h, tile * ROWS:(tile + 1) * ROWS, :] * chain[degree][z, h, at:at + ROWS, :]
                             - weight[z, tile] * box[h])
                    if degree == 0:
                        value = 0.5 * value
                    else:
                        value = value - chain[degree - 1][z, h, at:at + ROWS, :]
                    chain[degree + 1][z, h, at:at + ROWS, :] = value
                out.append((here, after))
            return tuple(out)
        init = tuple((row_sums(c[degree], start - 1, k), row_sums(c[degree], start, k)) for c, k in jobs)
        for z in range(start, stop):
            init = step(z, init)

    gl = lax.broadcasted_iota(jnp.int32, (2 * ROWS, LANES), 1)
    gr = lax.broadcasted_iota(jnp.int32, (2 * ROWS, LANES), 0)
    change = basis_change()
    diag_b = [change[i, i] for i in range(COLS)]
    low_b = [change[i, i - 1] if i else 0.0 for i in range(COLS)]
    up_b = [change[i, i + 1] if i < COLS - 1 else 0.0 for i in range(COLS)]
    b_row = [table(gl, v) for v in (diag_b, low_b, up_b)]
    b_col = [table(gr, v) for v in (diag_b, low_b, up_b)]

    b_down = [table(gl, v) for v in (
        diag_b, [change[j + 1, j] if j < COLS - 1 else 0.0 for j in range(COLS)],
        [change[j - 1, j] if j else 0.0 for j in range(COLS)])]

    def apply_b(col, row):
        q_row = b_row[0] * row + b_row[1] * pltpu.roll(row, 1, 1) + b_row[2] * pltpu.roll(row, LANES - 1, 1)
        q_col = b_col[0] * col + b_col[1] * pltpu.roll(col, 1, 0) + b_col[2] * pltpu.roll(col, 2 * ROWS - 1, 0)
        return q_col, q_row

    def outer(t, carry):
        for degree in range(S):
            if degree < S - 1:
                degree_sweep((p_at,), degree, degree + 1, ze - degree - 1, range(tiles))
                r_tiles = range(tiles) if degree < S - 2 else (1,)
                degree_sweep((r_at,), degree, degree + 2, ze - degree - 2, r_tiles)
            else:
                degree_sweep((p_at,), degree, degree + 1, ze - degree - 1, (1,))
        basis = p_at + r_at

        for lo_i, hi_i, lo_j in ((0, S + 1, 0), (0, S + 1, S + 1), (S + 1, COLS, S + 1)):
            hi_j = S + 1 if lo_j == 0 else COLS
            sums = {}
            for z in range(S, S + bz):
                for h in range(halves):
                    va = [basis[i][z, h, mid_y, :] for i in range(lo_i, hi_i)]
                    vb = va if lo_i == lo_j else [basis[j][z, h, mid_y, :] for j in range(lo_j, hi_j)]
                    for i in range(lo_i, hi_i):
                        for j in range(max(i, lo_j), hi_j):
                            term = va[i - lo_i] * vb[j - lo_j]
                            sums[i, j] = sums[i, j] + term if (i, j) in sums else term
            for (i, j), value in sums.items():
                line = jnp.sum(value, axis=0, keepdims=True)
                pairs[i * 16 + j:i * 16 + j + 1, :] = line
                if i != j:
                    pairs[j * 16 + i:j * 16 + i + 1, :] = line
        for half in range(2):
            turned = pairs[half * LANES:(half + 1) * LANES, :].T
            g_send[half:half + 1, :] = jnp.sum(turned, axis=0, keepdims=True)

        slot = t % 2
        turn = jnp.where(iz * 2 < nz, -1, 1)
        own = pltpu.make_async_copy(g_send, g_recv.at[slot, me], g_rsem.at[slot])
        own.start()

        def send(k, c):
            peer = (me + turn + turn * k + count) % count
            pltpu.make_async_remote_copy(
                src_ref=g_send, dst_ref=g_recv.at[slot, me],
                send_sem=g_ssem, recv_sem=g_rsem.at[slot],
                device_id=(peer // (ny * nx), (peer // nx) % ny, peer % nx), device_id_type=MESH).start()
            return c
        lax.fori_loop(0, count - 1, send, 0, unroll=4)
        everything = g_recv.at[slot]
        pltpu.make_async_copy(everything, everything, g_rsem.at[slot]).wait()
        most = g_recv.at[slot, 0:count - 1]
        pltpu.make_async_copy(most, most, g_ssem).wait()
        rows2 = jnp.sum(g_recv[slot], axis=0)
        gram = jnp.zeros((2 * ROWS, LANES), jnp.float32)
        for half in range(2):
            line = jnp.broadcast_to(rows2[half:half + 1, :], (2 * ROWS, LANES))
            for k in range(8):
                i = half * 8 + k
                if i < COLS:
                    moved = line if k == 0 else pltpu.roll(line, LANES - 16 * k, 1)
                    gram = jnp.where(gr == i, moved, gram)
        gram = jnp.where(gl < COLS, gram, 0.0)

        def quad(matrix, col, row):
            return jnp.sum(jnp.sum(matrix * col * row, axis=0, keepdims=True), axis=1, keepdims=True)

        moved_gram = (gram * b_down[0] + pltpu.roll(gram, LANES - 1, 1) * b_down[1] + pltpu.roll(gram, 1, 1) * b_down[2])

        p_row, p_col = (gl == 0).astype(jnp.float32), (gr == 0).astype(jnp.float32)
        r_row, r_col = (gl == S + 1).astype(jnp.float32), (gr == S + 1).astype(jnp.float32)
        x_col = jnp.zeros((2 * ROWS, LANES), jnp.float32)
        norm = quad(gram, r_col, r_row)
        for _ in range(S):
            q_col, q_row = apply_b(p_col, p_row)
            length = norm / quad(moved_gram, p_col, p_row)
            x_col = x_col + length * p_col
            r_col = r_col - length * q_col
            r_row = r_row - length * q_row
            fresh = quad(gram, r_col, r_row)
            ratio = fresh / norm
            p_col = r_col + ratio * p_col
            p_row = r_row + ratio * p_row
            norm = fresh

        def weights(col):
            return [jnp.broadcast_to(col[i:i + 1, :], (hy, LANES)) for i in range(COLS)]

        xw, rw, pw = weights(x_col), weights(r_col), weights(p_col)
        for z in range(bz):
            for h in range(halves):
                vs = [b[S + z, h, mid_y, :] for b in basis]

                def mix(w):
                    out = w[0] * vs[0]
                    for a, b in zip(w[1:], vs[1:]):
                        out = out + a * b
                    return out
                total[0, z, h] = total[0, z, h] + mix(xw)
                fields[0, S + z, h, mid_y, :] = mix(rw)
                fields[1, S + z, h, mid_y, :] = mix(pw)

        @pl.when(t < OUTER - 1)
        def _():
            exchange(0)
        return carry

    lax.fori_loop(0, OUTER, outer, 0)

    total[1] = fields[0, mid_z, :, mid_y, :]
    back = pltpu.make_async_remote_copy(
        src_ref=total.at[:, :, other], dst_ref=final,
        send_sem=swap_send.at[0], recv_sem=swap_recv.at[0],
        device_id=(iz, iy, other), device_id_type=MESH)
    back.start()
    for k, out in enumerate((sol_out, res_out)):
        out[:, row_tile(ix), :] = total[k, :, ix]
    back.wait()
    for k, out in enumerate((sol_out, res_out)):
        out[:, row_tile(other), :] = final[k]


def solution(mesh):
    nz, ny, nx = mesh.shape["gz"], mesh.shape["gy"], mesh.shape["gx"]
    count = nz * ny * nx

    def body(right_side, diagonal):
        bz, by, bx = right_side.shape
        hy = by // 2
        assert nx == 2 and bz >= S and hy == ROWS and bx == LANES
        ze, ye = bz + 2 * S, hy + 4 * ROWS
        f32, dma = jnp.float32, pltpu.SemaphoreType.DMA
        return pl.pallas_call(
            lambda *refs: kernel(nz, ny, nx, *refs),
            out_shape=(jax.ShapeDtypeStruct(right_side.shape, f32),) * 2,
            in_specs=[pl.BlockSpec(memory_space=pltpu.VMEM)] * 2,
            out_specs=(pl.BlockSpec(memory_space=pltpu.VMEM),) * 2,
            scratch_shapes=[
                pltpu.VMEM((3, ze, nx, ye, bx), f32),
                pltpu.VMEM((S, ze, nx, ye, bx), f32),
                pltpu.VMEM((S - 1, ze, nx, ye, bx), f32),
                pltpu.VMEM((ze, nx, hy + 2 * ROWS, bx), f32),
                pltpu.VMEM((ze, 3, ROWS, bx), f32),
                pltpu.VMEM((2, bz, nx, hy, bx), f32),
                pltpu.VMEM((2 * LANES, LANES), f32),
                pltpu.VMEM((2, LANES), f32),
                pltpu.VMEM((2, count, 2, LANES), f32),
                pltpu.VMEM((2, bz, hy, bx), f32),
                dma((2, 2)), dma((2, 2)), dma((2, 2, 3)), dma((2, 2, 3)),
                dma, dma((2,)), dma((2,)), dma((2,)), dma((2,)),
            ],
            compiler_params=pltpu.CompilerParams(has_side_effects=True),
        )(right_side, diagonal)

    spec = P("gz", "gy", "gx")
    return jax.shard_map(body, mesh=mesh, in_specs=(spec, spec), out_specs=(spec, spec), check_vma=False)
```

profile of v0, /device:TPU:1, one launch (start us, length us, event | category | flops | bytes accessed | tf_op | source)
XLA Modules:
  0.0 142.7 jit_solution(15023048389248455256)
XLA Ops:
  0.6 139.9 %shard_map.41 = (f32[8,16,128]{2,1,0:T(8,128)}, f32[8,16,128]{2,1,0:T(8,128)}) custom-call(f32[8,16,128]{2,1,0:T(8,128)} %refs_0_.1, f32[8,16,128]{2,1,0:T(8,128)} %refs_1_.1), custom_call_target="tpu_custom_call" | custom-call | tf_op jit(solution)/shard_map/pallas_call | solution.py:360
  140.6 0.0 copy-start
  140.6 1.5 %copy.6 = f32[8,16,128]{2,1,0:T(8,128)} copy(f32[8,16,128]{2,1,0:T(8,128)} %get-tuple-element.4) | data formatting | bytes 131072
  142.1 0.0 copy-done
  142.1 0.6 copy.7
Async XLA Ops:
  140.6 1.5 %copy-start = (f32[8,16,128]{2,1,0:T(8,128)S(1)}, f32[8,16,128]{2,1,0:T(8,128)}, u32[]{:S(2)}) copy-start(f32[8,16,128]{2,1,0:T(8,128)} %get-tuple-element.5) | copy-start | bytes 196612
where the time goes:
time: 145 us; the launch traced here: 143 us
  Pallas kernels  140 us (97%)
  local copies, waits for them, and re-layouts  2.14 us (1%)
    pallas_call x1, Pallas kernels, body(): pl.pallas_call(lambda *refs: kernel(nz, ny, nx, *refs), out_shape=(jax.Sh...  140 us

commit v1 on v0

v1 whole, which is shorter than its diff:
```python
import jax
import jax.numpy as jnp
from jax import lax
from jax.experimental import pallas as pl
from jax.experimental.pallas import tpu as pltpu
from jax.sharding import PartitionSpec as P

S = 6
OUTER = 5
ROUNDS = 3
DEG = S * OUTER // ROUNDS
HALO = DEG // 2
SHIFT = 19.0
HALF = 19.0
LANES = 128
ROWS = 8
BLOCK = 64
MESH = pl.DeviceIdType.MESH


def two_sum(a, b):
    s = a + b
    t = s - a
    return s, (a - (s - t)) + (b - t)


def pair_add(a, b):
    s, e = two_sum(a[0], b[0])
    e = e + (a[1] + b[1])
    h = s + e
    return h, e - (h - s)


def split(a):
    c = 4097.0 * a
    high = c - (c - a)
    return high, a - high


def pair_scale(a, b, b_parts):
    p = a[0] * b
    h, l = split(a[0])
    e = ((h * b_parts[0] - p) + h * b_parts[1] + l * b_parts[0]) + l * b_parts[1]
    e = e + a[1] * b
    s = p + e
    return s, e - (s - p)


def kernel(nz, ny, nx, rhs_ref, diag_ref, sol_out, res_out,
           fields, p_low, r_low, p_wave, r_wave, p_high, r_high, scale2, weight, total, pairs,
           a_send, a_recv, b_send, b_recv, final,
           z_send, z_recv, y_send, y_recv, a_ssem, a_rsem, b_ssem, b_rsem, swap_send, swap_recv, own_sem):
    bz, by, bx = rhs_ref.shape
    hy = by // 2
    ze, halves, ya = fields.shape[1:4]
    first = (ya - hy) // 2
    low_rows, high_rows = slice(first - ROWS, first), slice(first + hy, first + hy + ROWS)
    iz, iy, ix = lax.axis_index("gz"), lax.axis_index("gy"), lax.axis_index("gx")
    other = 1 - ix
    yy = iy * 2 + ix
    has_z = (iz > 0, iz < nz - 1)
    has_y = (yy > 0, yy < 2 * ny - 1)
    z_dev = tuple((iz + s, iy, ix) for s in (-1, 1))
    y_dev = tuple((iz, (yy + s) // 2, other) for s in (-1, 1))
    mid_z, mid_y = slice(HALO, HALO + bz), slice(first, first + hy)
    RES, DIR, DIA, DIR5, RES5 = range(5)

    def row_tile(index):
        return pl.ds(pl.multiple_of(index * hy, hy), hy)

    swaps, owns = [], []
    for k, (ref, field) in enumerate(((rhs_ref, DIR), (diag_ref, DIA))):
        spot = fields.at[field, mid_z, ix, mid_y, :]
        swap = pltpu.make_async_remote_copy(
            src_ref=ref.at[:, row_tile(other), :], dst_ref=spot,
            send_sem=swap_send.at[k], recv_sem=swap_recv.at[k],
            device_id=(iz, iy, other), device_id_type=MESH)
        swap.start()
        own = pltpu.make_async_copy(ref.at[:, row_tile(ix), :], spot, own_sem.at[k])
        own.start()
        swaps.append(swap)
        owns.append(own)

    for side in range(2):
        planes = slice(0, HALO) if side == 0 else slice(HALO + bz, ze)
        rows = (low_rows, high_rows)[side]

        @pl.when(jnp.logical_not(has_z[side]))
        def _():
            for k in range(5):
                fields[k, planes] = jnp.zeros((HALO, halves, ya, bx), jnp.float32)

        @pl.when(jnp.logical_not(has_y[side]))
        def _():
            for k in range(5):
                fields[k, :, :, rows, :] = jnp.zeros((ze, halves, ROWS, bx), jnp.float32)

    w_unit = 2.0 / HALF
    w_low = jnp.where(has_y[0], jnp.float32(w_unit), 0.0)
    w_high = jnp.where(has_y[1], jnp.float32(w_unit), 0.0)
    z_low = jnp.where(has_z[0], jnp.float32(1.0), 0.0)
    z_high = jnp.where(has_z[1], jnp.float32(1.0), 0.0)
    for plane in range(ze):
        factor = z_low if plane < HALO else (z_high if plane >= HALO + bz else jnp.float32(1.0))
        for tile, w in enumerate((w_low, jnp.float32(w_unit), w_high)):
            weight[plane, tile] = jnp.broadcast_to(w * factor, (ROWS, bx))
    total[...] = jnp.zeros(total.shape, jnp.float32)
    pairs[...] = jnp.zeros(pairs.shape, jnp.float32)

    for copy in owns + swaps:
        copy.wait()

    def z_copy(item, side):
        field, depth, k = item
        low_src, high_src = slice(HALO, HALO + depth), slice(HALO + bz - depth, HALO + bz)
        low_dst, high_dst = slice(HALO - depth, HALO), slice(HALO + bz, HALO + bz + depth)
        src, dst = ((low_src, high_dst), (high_src, low_dst))[side]
        return pltpu.make_async_remote_copy(
            src_ref=fields.at[field, src, :, mid_y, :], dst_ref=fields.at[field, dst, :, mid_y, :],
            send_sem=z_send.at[k, side], recv_sem=z_recv.at[k, 1 - side],
            device_id=z_dev[side], device_id_type=MESH)

    def y_copy(item, side, part):
        field, depth, k = item
        planes = (mid_z, slice(HALO - depth, HALO), slice(HALO + bz, HALO + bz + depth))[part]
        low_src, high_src = slice(first, first + depth), slice(first + hy - depth, first + hy)
        low_dst, high_dst = slice(first - depth, first), slice(first + hy, first + hy + depth)
        src, dst = ((low_src, high_dst), (high_src, low_dst))[side]
        return pltpu.make_async_remote_copy(
            src_ref=fields.at[field, planes, :, src, :], dst_ref=fields.at[field, planes, :, dst, :],
            send_sem=y_send.at[k, side, part], recv_sem=y_recv.at[k, 1 - side, part],
            device_id=y_dev[side], device_id_type=MESH)

    def exchange(items):
        for item in items:
            for side in range(2):
                @pl.when(has_z[side])
                def _():
                    z_copy(item, side).start()
        for item in items:
            for side in range(2):
                @pl.when(has_y[side])
                def _():
                    y_copy(item, side, 0).start()
        for item in items:
            for z_side in range(2):
                @pl.when(has_z[z_side])
                def _():
                    z_copy(item, 1 - z_side).wait_recv()
                    for side in range(2):
                        @pl.when(has_y[side])
                        def _():
                            y_copy(item, side, 1 + z_side).start()
        for item in items:
            for side in range(2):
                @pl.when(has_z[side])
                def _():
                    z_copy(item, side).wait_send()

                @pl.when(has_y[side])
                def _():
                    y_copy(item, side, 0).wait_send()
                    y_copy(item, 1 - side, 0).wait_recv()
                    for z_side in range(2):
                        @pl.when(has_z[z_side])
                        def _():
                            y_copy(item, side, 1 + z_side).wait_send()
                            y_copy(item, 1 - side, 1 + z_side).wait_recv()

    exchange(((DIR, HALO, 0), (DIA, HALO - 1, 1)))
    all_rows = slice(first - ROWS, first + hy + ROWS)

    def prepare(plane, c):
        scale2[plane] = (fields[DIA, plane, :, all_rows, :] + (27.0 - SHIFT)) * (2.0 / HALF)
        return c
    lax.fori_loop(0, ze, prepare, 0)

    tiles = (hy + 2 * ROWS) // ROWS
    lane_id = lax.broadcasted_iota(jnp.int32, (ROWS, bx), 1)
    first_lane, last_lane = lane_id == 0, lane_id == bx - 1

    def row_sums(ref, z, tile):
        at = first - ROWS + tile * ROWS
        return [ref[z, h, at - 1:at - 1 + ROWS, :] + ref[z, h, at:at + ROWS, :] + ref[z, h, at + 1:at + 1 + ROWS, :]
                for h in range(halves)]

    def lane_sums(parts):
        left = [pltpu.roll(v, 1, 1) for v in parts]
        right = [pltpu.roll(v, bx - 1, 1) for v in parts]
        out = []
        for h in range(halves):
            before = left[h - 1] if h else 0.0
            after = right[h + 1] if h < halves - 1 else 0.0
            out.append(parts[h] + jnp.where(first_lane, before, left[h]) + jnp.where(last_lane, after, right[h]))
        return out

    p_at = [fields.at[DIR]] + [p_low.at[k] for k in range(HALO - 1)] + [fields.at[DIR5]]
    r_at = [fields.at[RES]] + [r_low.at[k] for k in range(HALO - 1)] + [fields.at[RES5]]
    p_on = [fields.at[DIR5]] + [p_wave.at[k] for k in range(HALO)]
    r_on = [fields.at[RES5]] + [r_wave.at[k] for k in range(HALO - 1)]

    def sweep(chain, degree, depth):
        start, stop = HALO - depth, HALO + bz + depth
        chosen = range(tiles) if depth else (1,)

        def step(z, carry):
            out = []
            for tile, (before, here) in zip(chosen, carry):
                after = row_sums(chain[degree], z + 1, tile)
                box = lane_sums([a + b + c for a, b, c in zip(before, here, after)])
                at = first - ROWS + tile * ROWS
                for h in range(halves):
                    value = (scale2[z, h, tile * ROWS:(tile + 1) * ROWS, :] * chain[degree][z, h, at:at + ROWS, :]
                             - weight[z, tile] * box[h])
                    if degree == 0:
                        value = 0.5 * value
                    else:
                        value = value - chain[degree - 1][z, h, at:at + ROWS, :]
                    chain[degree + 1][z, h, at:at + ROWS, :] = value
                out.append((here, after))
            return tuple(out)
        carry = tuple((row_sums(chain[degree], start - 1, k), row_sums(chain[degree], start, k)) for k in chosen)
        for z in range(start, stop):
            carry = step(z, carry)

    gl = lax.broadcasted_iota(jnp.int32, (ROWS, LANES), 1)
    zero_lane, up_twice = gl == 0, jnp.where((gl == 1) | (gl == BLOCK + 1), jnp.float32(2.0), jnp.float32(1.0))
    in_block = (gl <= DEG) | ((gl >= BLOCK) & (gl <= BLOCK + DEG))

    def pick(v, lane):
        return jnp.broadcast_to(v[:, lane:lane + 1], (ROWS, LANES))

    def moved(pair):
        up = [pltpu.roll(v, LANES - 1, 1) for v in pair]
        down = [jnp.where(zero_lane, u, pltpu.roll(v, 1, 1)) for u, v in zip(up, pair)]
        return pair_add((2.0 * pair[0], 2.0 * pair[1]), pair_add(up, down))

    def apply_b(c):
        return jnp.where(in_block, 2.0 * c + up_twice * pltpu.roll(c, 1, 1) + pltpu.roll(c, LANES - 1, 1), 0.0)

    def everywhere(row, slot):
        a_me, b_me = yy, iz
        a_count, b_count = ny * nx, nz

        def stage(send_ref, recv_ref, me, count, ssem, rsem, dev, value):
            send_ref[...] = value
            recv_ref[slot, me] = value
            for k in range(1, count):
                peer = (me + k) % count
                pltpu.make_async_remote_copy(
                    src_ref=send_ref, dst_ref=recv_ref.at[slot, me],
                    send_sem=ssem, recv_sem=rsem.at[slot],
                    device_id=dev(peer), device_id_type=MESH).start()
            most = recv_ref.at[slot, 0:count - 1]
            pltpu.make_async_copy(most, most, rsem.at[slot]).wait()
            out = jnp.sum(recv_ref[slot], axis=0)
            pltpu.make_async_copy(most, most, ssem).wait()
            return out
        mine = stage(a_send, a_recv, a_me, a_count, a_ssem, a_rsem, lambda p: (iz, p // nx, p % nx), row)
        return stage(b_send, b_recv, b_me, b_count, b_ssem, b_rsem, lambda p: (p, iy, ix), mine)

    def outer(t, two):
        for degree in range(HALO):
            sweep(p_at, degree, HALO - 1 - degree)
            if two:
                sweep(r_at, degree, HALO - 1 - degree)
        exchange(((DIR5, HALO, 2), (RES5, HALO - 1, 3)) if two else ((DIR5, HALO, 2),))
        for degree in range(HALO):
            sweep(p_on, degree, HALO - 1 - degree)
            if two and degree < HALO - 1:
                sweep(r_on, degree, HALO - 2 - degree)

        sums = {}

        def add(key, value):
            sums[key] = sums[key] + value if key in sums else value
        for z in range(bz):
            for h in range(halves):
                here = (HALO + z, h, mid_y, slice(None))
                lists = []
                for low, wave, high in ((p_at, p_on, p_high), (r_at, r_on, r_high))[:1 + two]:
                    vs = [ref[here] for ref in low]
                    for k in range(1, len(wave)):
                        value = 2.0 * wave[k][here] - vs[HALO - k]
                        high[k - 1, z, h] = value
                        vs.append(value)
                    lists.append(vs)
                ps = lists[0]
                for k in range(2 * DEG + 1):
                    add(k, ps[(k + 1) // 2] * ps[k // 2])
                if two:
                    rs = lists[1]
                    for k in range(2 * DEG):
                        add(BLOCK + k, ps[(k + 1) // 2] * rs[k // 2])
        lines = {}
        for key, value in sums.items():
            base = key // BLOCK * BLOCK
            if key - base > 1:
                value = 2.0 * value - sums[base + (key - base) % 2]
            pairs[key:key + 1, :] = jnp.sum(value, axis=0, keepdims=True)
        row = jnp.sum(pairs[...].T, axis=0, keepdims=True)
        row = jnp.broadcast_to(everywhere(row, t), (ROWS, LANES))

        nil = jnp.zeros((ROWS, LANES), jnp.float32)
        pi = (row, nil)
        rho = (pltpu.roll(row, LANES - BLOCK, 1), nil) if two else pi
        p_c = (gl == 0).astype(jnp.float32)
        r_c = (gl == BLOCK).astype(jnp.float32) if two else p_c
        x_c = nil
        rho_k = pick(rho[0], 0)
        for k in range(DEG):
            q = moved(pi)
            length = rho_k / pick(q[0], k)
            less = -length
            change = pair_scale(q, less, split(less))
            rho = pair_add(rho, change)
            fresh = pick(rho[0], k + 1)
            ratio = (-2.0 if k == 0 else -1.0) * length * (fresh / rho_k)
            pi = pair_add(rho, pair_scale(pi, ratio, split(ratio)))
            rho_k = fresh
            q_c = apply_b(p_c)
            x_c = x_c + (length * (2.0 / HALF)) * p_c
            r_c = r_c - length * q_c
            p_c = r_c + ratio * p_c

        lanes = list(range(DEG + 1)) + (list(range(BLOCK, BLOCK + DEG)) if two else [])
        xw, rw, pw = ([pick(c, lane) for lane in lanes] for c in (x_c, r_c, p_c))
        for z in range(bz):
            for h in range(halves):
                here = (HALO + z, h, mid_y, slice(None))
                vs = [ref[here] for ref in p_at] + [p_high[k, z, h] for k in range(HALO)]
                if two:
                    vs += [ref[here] for ref in r_at] + [r_high[k, z, h] for k in range(HALO - 1)]

                def mix(w):
                    out = w[0] * vs[0]
                    for a, b in zip(w[1:], vs[1:]):
                        out = out + a * b
                    return out
                total[0, z, h] = total[0, z, h] + mix(xw)
                fields[RES, HALO + z, h, mid_y, :] = mix(rw)
                fields[DIR, HALO + z, h, mid_y, :] = mix(pw)

    outer(0, False)

    def later(t, carry):
        exchange(((DIR, HALO, 0), (RES, HALO, 1)))
        outer(t, True)
        return carry
    lax.fori_loop(1, ROUNDS, later, 0)

    total[1] = fields[RES, mid_z, :, mid_y, :]
    back = pltpu.make_async_remote_copy(
        src_ref=total.at[:, :, other], dst_ref=final,
        send_sem=swap_send.at[0], recv_sem=swap_recv.at[0],
        device_id=(iz, iy, other), device_id_type=MESH)
    back.start()
    for k, out in enumerate((sol_out, res_out)):
        out[:, row_tile(ix), :] = total[k, :, ix]
    back.wait()
    for k, out in enumerate((sol_out, res_out)):
        out[:, row_tile(other), :] = final[k]


def solution(mesh):
    nz, ny, nx = mesh.shape["gz"], mesh.shape["gy"], mesh.shape["gx"]

    def body(right_side, diagonal):
        bz, by, bx = right_side.shape
        hy = by // 2
        assert nx == 2 and bz >= HALO and hy == ROWS and bx == LANES
        ze, ye = bz + 2 * HALO, hy + 4 * ROWS
        f32, dma = jnp.float32, pltpu.SemaphoreType.DMA
        return pl.pallas_call(
            lambda *refs: kernel(nz, ny, nx, *refs),
            out_shape=(jax.ShapeDtypeStruct(right_side.shape, f32),) * 2,
            in_specs=[pl.BlockSpec(memory_space=pltpu.VMEM)] * 2,
            out_specs=(pl.BlockSpec(memory_space=pltpu.VMEM),) * 2,
            scratch_shapes=[
                pltpu.VMEM((5, ze, nx, ye, bx), f32),
                pltpu.VMEM((HALO - 1, ze, nx, ye, bx), f32),
                pltpu.VMEM((HALO - 1, ze, nx, ye, bx), f32),
                pltpu.VMEM((HALO, ze, nx, ye, bx), f32),
                pltpu.VMEM((HALO - 1, ze, nx, ye, bx), f32),
                pltpu.VMEM((HALO, bz, nx, hy, bx), f32),
                pltpu.VMEM((HALO - 1, bz, nx, hy, bx), f32),
                pltpu.VMEM((ze, nx, hy + 2 * ROWS, bx), f32),
                pltpu.VMEM((ze, 3, ROWS, bx), f32),
                pltpu.VMEM((2, bz, nx, hy, bx), f32),
                pltpu.VMEM((LANES, LANES), f32),
                pltpu.VMEM((1, LANES), f32),
                pltpu.VMEM((ROUNDS, ny * nx, 1, LANES), f32),
                pltpu.VMEM((1, LANES), f32),
                pltpu.VMEM((ROUNDS, nz, 1, LANES), f32),
                pltpu.VMEM((2, bz, hy, bx), f32),
                dma((4, 2)), dma((4, 2)), dma((4, 2, 3)), dma((4, 2, 3)),
                dma, dma((ROUNDS,)), dma, dma((ROUNDS,)),
                dma((2,)), dma((2,)), dma((2,)),
            ],
            compiler_params=pltpu.CompilerParams(has_side_effects=True),
        )(right_side, diagonal)

    spec = P("gz", "gy", "gx")
    return jax.shard_map(body, mesh=mesh, in_specs=(spec, spec), out_specs=(spec, spec), check_vma=False)
```

time: 145 us -> 109 us (0.75); the launches traced: 143 us -> 109 us
  Pallas kernels: 140 us -> 106 us
    pallas_call x1, Pallas kernels: 140 us -> 106 us  [body(): pl.pallas_call(lambda *refs: kernel(nz, ny, nx, *refs), out_shape=(jax.Sh...]
where the time goes in v1:
time: 109 us
  Pallas kernels  106 us (97%)
  local copies, waits for them, and re-layouts  2.14 us (2%)
    pallas_call x1, Pallas kernels, body(): pl.pallas_call(lambda *refs: kernel(nz, ny, nx, *refs), out_shape=(jax.Sh...  106 us

profile of v1, /device:TPU:1, one launch (start us, length us, event | category | flops | bytes accessed | tf_op | source)
XLA Modules:
  0.0 109.2 jit_solution(942391423414026973)
XLA Ops:
  0.6 106.4 %shard_map.41 = (f32[8,16,128]{2,1,0:T(8,128)}, f32[8,16,128]{2,1,0:T(8,128)}) custom-call(f32[8,16,128]{2,1,0:T(8,128)} %refs_0_.1, f32[8,16,128]{2,1,0:T(8,128)} %refs_1_.1), custom_call_target="tpu_custom_call" | custom-call | tf_op jit(solution)/shard_map/pallas_call | solution.py:374
  107.1 0.0 copy-start
  107.1 1.5 %copy.6 = f32[8,16,128]{2,1,0:T(8,128)} copy(f32[8,16,128]{2,1,0:T(8,128)} %get-tuple-element.4) | data formatting | bytes 131072
  108.6 0.0 copy-done
  108.6 0.6 copy.7
Async XLA Ops:
  107.1 1.5 %copy-start = (f32[8,16,128]{2,1,0:T(8,128)S(1)}, f32[8,16,128]{2,1,0:T(8,128)}, u32[]{:S(2)}) copy-start(f32[8,16,128]{2,1,0:T(8,128)} %get-tuple-element.5) | copy-start | bytes 196612

commit v2 on v1

--- a/solution.py
+++ b/solution.py
@@ -48,7 +48,7 @@
 
 def kernel(nz, ny, nx, rhs_ref, diag_ref, sol_out, res_out,
            fields, p_low, r_low, p_wave, r_wave, p_high, r_high, scale2, weight, total, pairs,
-           a_send, a_recv, b_send, b_recv, final,
+           a_send, a_recv, b_send, b_recv,
            z_send, z_recv, y_send, y_recv, a_ssem, a_rsem, b_ssem, b_rsem, swap_send, swap_recv, own_sem):
     bz, by, bx = rhs_ref.shape
     hy = by // 2
@@ -68,17 +68,18 @@
     def row_tile(index):
         return pl.ds(pl.multiple_of(index * hy, hy), hy)
 
-    swaps, owns = [], []
-    for k, (ref, field) in enumerate(((rhs_ref, DIR), (diag_ref, DIA))):
-        spot = fields.at[field, mid_z, ix, mid_y, :]
-        swap = pltpu.make_async_remote_copy(
-            src_ref=ref.at[:, row_tile(other), :], dst_ref=spot,
-            send_sem=swap_send.at[k], recv_sem=swap_recv.at[k],
-            device_id=(iz, iy, other), device_id_type=MESH)
-        swap.start()
+    barrier = pltpu.get_barrier_semaphore()
+    for k in range(1, ny * nx):
+        peer = (yy + k) % (ny * nx)
+        pl.semaphore_signal(barrier, inc=1, device_id=(iz, peer // nx, peer % nx), device_id_type=MESH)
+    for k in range(1, nz):
+        pl.semaphore_signal(barrier, inc=1, device_id=((iz + k) % nz, iy, ix), device_id_type=MESH)
+
+    owns = []
+    spots = [(ref, fields.at[field, mid_z, ix, mid_y, :]) for ref, field in ((rhs_ref, DIR), (diag_ref, DIA))]
+    for k, (ref, spot) in enumerate(spots):
         own = pltpu.make_async_copy(ref.at[:, row_tile(ix), :], spot, own_sem.at[k])
         own.start()
-        swaps.append(swap)
         owns.append(own)
 
     for side in range(2):
@@ -107,6 +108,15 @@
     total[...] = jnp.zeros(total.shape, jnp.float32)
     pairs[...] = jnp.zeros(pairs.shape, jnp.float32)
 
+    pl.semaphore_wait(barrier, ny * nx - 1 + nz - 1)
+    swaps = []
+    for k, (ref, spot) in enumerate(spots):
+        swap = pltpu.make_async_remote_copy(
+            src_ref=ref.at[:, row_tile(other), :], dst_ref=spot,
+            send_sem=swap_send.at[k], recv_sem=swap_recv.at[k],
+            device_id=(iz, iy, other), device_id_type=MESH)
+        swap.start()
+        swaps.append(swap)
     for copy in owns + swaps:
         copy.wait()
 
@@ -350,16 +360,17 @@
     lax.fori_loop(1, ROUNDS, later, 0)
 
     total[1] = fields[RES, mid_z, :, mid_y, :]
-    back = pltpu.make_async_remote_copy(
-        src_ref=total.at[:, :, other], dst_ref=final,
-        send_sem=swap_send.at[0], recv_sem=swap_recv.at[0],
-        device_id=(iz, iy, other), device_id_type=MESH)
-    back.start()
+    copies = []
     for k, out in enumerate((sol_out, res_out)):
-        out[:, row_tile(ix), :] = total[k, :, ix]
-    back.wait()
-    for k, out in enumerate((sol_out, res_out)):
-        out[:, row_tile(other), :] = final[k]
+        copies.append(pltpu.make_async_remote_copy(
+            src_ref=total.at[k, :, other], dst_ref=out.at[:, row_tile(ix), :],
+            send_sem=swap_send.at[k], recv_sem=swap_recv.at[k],
+            device_id=(iz, iy, other), device_id_type=MESH))
+        copies.append(pltpu.make_async_copy(total.at[k, :, ix], out.at[:, row_tile(ix), :], own_sem.at[k]))
+    for copy in copies:
+        copy.start()
+    for copy in copies:
+        copy.wait()
 
 
 def solution(mesh):
@@ -374,8 +385,8 @@
         return pl.pallas_call(
             lambda *refs: kernel(nz, ny, nx, *refs),
             out_shape=(jax.ShapeDtypeStruct(right_side.shape, f32),) * 2,
-            in_specs=[pl.BlockSpec(memory_space=pltpu.VMEM)] * 2,
-            out_specs=(pl.BlockSpec(memory_space=pltpu.VMEM),) * 2,
+            in_specs=[pl.BlockSpec(memory_space=pl.ANY)] * 2,
+            out_specs=(pl.BlockSpec(memory_space=pl.ANY),) * 2,
             scratch_shapes=[
                 pltpu.VMEM((5, ze, nx, ye, bx), f32),
                 pltpu.VMEM((HALO - 1, ze, nx, ye, bx), f32),
@@ -392,12 +403,11 @@
                 pltpu.VMEM((ROUNDS, ny * nx, 1, LANES), f32),
                 pltpu.VMEM((1, LANES), f32),
                 pltpu.VMEM((ROUNDS, nz, 1, LANES), f32),
-                pltpu.VMEM((2, bz, hy, bx), f32),
                 dma((4, 2)), dma((4, 2)), dma((4, 2, 3)), dma((4, 2, 3)),
                 dma, dma((ROUNDS,)), dma, dma((ROUNDS,)),
                 dma((2,)), dma((2,)), dma((2,)),
             ],
-            compiler_params=pltpu.CompilerParams(has_side_effects=True),
+            compiler_params=pltpu.CompilerParams(collective_id=0, has_side_effects=True),
         )(right_side, diagonal)
 
     spec = P("gz", "gy", "gx")

time: 109 us -> 100 us (0.917)
  Pallas kernels: 106 us -> 97.1 us
    pallas_call x1, Pallas kernels: 106 us -> 97.1 us  [body(): pl.pallas_call(lambda *refs: kernel(nz, ny, nx, *refs), out_shape=(jax.Sh...]
where the time goes in v2:
time: 100 us; the launch traced here: 99.9 us
  Pallas kernels  97.1 us (97%)
  local copies, waits for them, and re-layouts  2.14 us (2%)
    pallas_call x1, Pallas kernels, body(): pl.pallas_call(lambda *refs: kernel(nz, ny, nx, *refs), out_shape=(jax.Sh...  97.1 us
    unnamed x4, local copies, waits for them, and re-layouts  2.14 us

profile of v2, /device:TPU:1, one launch (start us, length us, event | category | flops | bytes accessed | tf_op | source)
XLA Modules:
  0.0 99.9 jit_solution(17603576996066081659)
XLA Ops:
  0.6 97.1 %shard_map.41 = (f32[8,16,128]{2,1,0:T(8,128)}, f32[8,16,128]{2,1,0:T(8,128)}) custom-call(f32[8,16,128]{2,1,0:T(8,128)} %refs_0_.1, f32[8,16,128]{2,1,0:T(8,128)} %refs_1_.1), custom_call_target="tpu_custom_call" | custom-call | tf_op jit(solution)/shard_map/pallas_call | solution.py:385
  97.8 0.0 copy-start
  97.8 1.5 %copy.6 = f32[8,16,128]{2,1,0:T(8,128)} copy(f32[8,16,128]{2,1,0:T(8,128)} %get-tuple-element.4) | data formatting | bytes 131072
  99.3 0.0 copy-done
  99.3 0.6 copy.7
Async XLA Ops:
  97.8 1.5 %copy-start = (f32[8,16,128]{2,1,0:T(8,128)S(1)}, f32[8,16,128]{2,1,0:T(8,128)}, u32[]{:S(2)}) copy-start(f32[8,16,128]{2,1,0:T(8,128)} %get-tuple-element.5) | copy-start | bytes 196612

commit v3 on v2

--- a/solution.py
+++ b/solution.py
@@ -317,16 +317,17 @@
         p_c = (gl == 0).astype(jnp.float32)
         r_c = (gl == BLOCK).astype(jnp.float32) if two else p_c
         x_c = nil
+        q = moved(pi)
         rho_k = pick(rho[0], 0)
         for k in range(DEG):
-            q = moved(pi)
-            length = rho_k / pick(q[0], k)
+            inverse = 1.0 / pick(q[0], k)
+            length = rho_k * inverse
             less = -length
-            change = pair_scale(q, less, split(less))
-            rho = pair_add(rho, change)
+            rho = pair_add(rho, pair_scale(q, less, split(less)))
             fresh = pick(rho[0], k + 1)
-            ratio = (-2.0 if k == 0 else -1.0) * length * (fresh / rho_k)
-            pi = pair_add(rho, pair_scale(pi, ratio, split(ratio)))
+            ratio = ((-2.0 if k == 0 else -1.0) * inverse) * fresh
+            if k < DEG - 1:
+                q = pair_add(moved(rho), pair_scale(q, ratio, split(ratio)))
             rho_k = fresh
             q_c = apply_b(p_c)
             x_c = x_c + (length * (2.0 / HALF)) * p_c

time: 100 us -> 98 us (0.980)
  Pallas kernels: 97.1 us -> 95.1 us
    pallas_call x1, Pallas kernels: 97.1 us -> 95.1 us  [body(): pl.pallas_call(lambda *refs: kernel(nz, ny, nx, *refs), out_shape=(jax.Sh...]
where the time goes in v3:
time: 98 us; the launch traced here: 97.8 us
  Pallas kernels  95.1 us (97%)
  local copies, waits for them, and re-layouts  2.14 us (2%)
    pallas_call x1, Pallas kernels, body(): pl.pallas_call(lambda *refs: kernel(nz, ny, nx, *refs), out_shape=(jax.Sh...  95.1 us
    unnamed x4, local copies, waits for them, and re-layouts  2.14 us

profile of v3, /device:TPU:1, one launch (start us, length us, event | category | flops | bytes accessed | tf_op | source)
XLA Modules:
  0.0 97.8 jit_solution(10706603609319757171)
XLA Ops:
  0.6 95.1 %shard_map.41 = (f32[8,16,128]{2,1,0:T(8,128)}, f32[8,16,128]{2,1,0:T(8,128)}) custom-call(f32[8,16,128]{2,1,0:T(8,128)} %refs_0_.1, f32[8,16,128]{2,1,0:T(8,128)} %refs_1_.1), custom_call_target="tpu_custom_call" | custom-call | tf_op jit(solution)/shard_map/pallas_call | solution.py:386
  95.7 0.0 copy-start
  95.7 1.5 %copy.6 = f32[8,16,128]{2,1,0:T(8,128)} copy(f32[8,16,128]{2,1,0:T(8,128)} %get-tuple-element.4) | data formatting | bytes 131072
  97.2 0.0 copy-done
  97.2 0.6 copy.7
Async XLA Ops:
  95.7 1.5 %copy-start = (f32[8,16,128]{2,1,0:T(8,128)S(1)}, f32[8,16,128]{2,1,0:T(8,128)}, u32[]{:S(2)}) copy-start(f32[8,16,128]{2,1,0:T(8,128)} %get-tuple-element.5) | copy-start | bytes 196612

commit v4 on v3

--- a/solution.py
+++ b/solution.py
@@ -255,7 +255,7 @@
         def stage(send_ref, recv_ref, me, count, ssem, rsem, dev, value):
             send_ref[...] = value
             recv_ref[slot, me] = value
-            for k in range(1, count):
+            for k in sorted(range(1, count), key=lambda k: -min(k % 8, 8 - k % 8) - 2 * min(k // 8, (count - k) // 8)):
                 peer = (me + k) % count
                 pltpu.make_async_remote_copy(
                     src_ref=send_ref, dst_ref=recv_ref.at[slot, me],
@@ -263,11 +263,13 @@
                     device_id=dev(peer), device_id_type=MESH).start()
             most = recv_ref.at[slot, 0:count - 1]
             pltpu.make_async_copy(most, most, rsem.at[slot]).wait()
-            out = jnp.sum(recv_ref[slot], axis=0)
+            return jnp.sum(recv_ref[slot], axis=0)
+        mine = stage(a_send, a_recv, a_me, a_count, a_ssem, a_rsem, lambda p: (iz, p // nx, p % nx), row)
+        out = stage(b_send, b_recv, b_me, b_count, b_ssem, b_rsem, lambda p: (p, iy, ix), mine)
+        for recv_ref, count, ssem in ((a_recv, a_count, a_ssem), (b_recv, b_count, b_ssem)):
+            most = recv_ref.at[slot, 0:count - 1]
             pltpu.make_async_copy(most, most, ssem).wait()
-            return out
-        mine = stage(a_send, a_recv, a_me, a_count, a_ssem, a_rsem, lambda p: (iz, p // nx, p % nx), row)
-        return stage(b_send, b_recv, b_me, b_count, b_ssem, b_rsem, lambda p: (p, iy, ix), mine)
+        return out
 
     def outer(t, two):
         for degree in range(HALO):

time: 98 us -> 97.6 us (level)
  no operation moved by 1% of the time
where the time goes in v4:
time: 97.6 us; the launch traced here: 97.4 us
  Pallas kernels  94.7 us (97%)
  local copies, waits for them, and re-layouts  2.14 us (2%)
    pallas_call x1, Pallas kernels, body(): pl.pallas_call(lambda *refs: kernel(nz, ny, nx, *refs), out_shape=(jax.Sh...  94.7 us
    unnamed x4, local copies, waits for them, and re-layouts  2.14 us

profile of v4, /device:TPU:1, one launch (start us, length us, event | category | flops | bytes accessed | tf_op | source)
XLA Modules:
  0.0 97.4 jit_solution(9378557739384884563)
XLA Ops:
  0.6 94.7 %shard_map.41 = (f32[8,16,128]{2,1,0:T(8,128)}, f32[8,16,128]{2,1,0:T(8,128)}) custom-call(f32[8,16,128]{2,1,0:T(8,128)} %refs_0_.1, f32[8,16,128]{2,1,0:T(8,128)} %refs_1_.1), custom_call_target="tpu_custom_call" | custom-call | tf_op jit(solution)/shard_map/pallas_call | solution.py:388
  95.3 0.0 copy-start
  95.3 1.5 %copy.6 = f32[8,16,128]{2,1,0:T(8,128)} copy(f32[8,16,128]{2,1,0:T(8,128)} %get-tuple-element.4) | data formatting | bytes 131072
  96.8 0.0 copy-done
  96.8 0.6 copy.7
Async XLA Ops:
  95.3 1.5 %copy-start = (f32[8,16,128]{2,1,0:T(8,128)S(1)}, f32[8,16,128]{2,1,0:T(8,128)}, u32[]{:S(2)}) copy-start(f32[8,16,128]{2,1,0:T(8,128)} %get-tuple-element.5) | copy-start | bytes 196612
